TPU v7x, 32 devices: a whole 2x2x4 slice. The times are simulated.
32 devices in a mesh: rows: 8 (over y, x, core), grp: 4 (over z).
Axes of the slice: x: 2, y: 2, z: 4, core: 2. Of those that a mesh axis runs over, the one named last changes fastest.
Arguments:
- factor: float32 [8192, 1024], P(('rows', 'grp')), as said below
- start_block: float32 [1024, 256], replicated, may hold values from -6 to 6
Outputs:
- compressed: float32 [8192, 256], P(('rows', 'grp'))
- tail_share: float32 [], replicated
Inputs may be any that keep to these rules, and one draw needn't show every extreme that they name: Every entry is finite; the factor has full column rank.
All inputs are finite; a program needn't handle non-finite values.
Results may differ from a plain program's by a relative error of at most 0.0007.
Values sent between devices are 32-bit elements; how exact they have to be, the bound alone decides.
No kernel may reach another device: no remote copies, remote signals or barrier semaphores. Data moves between devices by JAX's collectives and lax.ppermute only.
A program may use at most 64 MiB of HBM per device.

v0:
```python
import functools
import math
import jax
import jax.numpy as jnp
from jax import lax
from jax.experimental import pallas as pl
from jax.experimental.pallas import tpu as pltpu
from jax.sharding import PartitionSpec as P

LANES = 128
PANEL = 32
STRIP = 16
EXACT = lax.Precision.HIGHEST
VMEM = pl.BlockSpec(memory_space=pltpu.VMEM)
HBM = pl.BlockSpec(memory_space=pltpu.HBM)


def dot(a, b, contract=((1,), (0,))):
    return lax.dot_general(
        a, b, (contract, ((), ())), precision=EXACT, preferred_element_type=jnp.float32
    )


def split3(x):
    high = x.astype(jnp.bfloat16)
    rest = x - high.astype(jnp.float32)
    mid = rest.astype(jnp.bfloat16)
    low = (rest - mid.astype(jnp.float32)).astype(jnp.bfloat16)
    return high, mid, low


def eliminate(m, out, n, first, last, lower, cols):
    width = m.shape[1]
    b = PANEL
    group = lax.broadcasted_iota(jnp.int32, (8, LANES), 0)
    for r0 in range(first, last, b):
        lo = r0 // LANES * LANES
        end = n + lo + LANES if lower else width
        chunks = list(range(lo, end, LANES))
        solved = [[] for _ in chunks]
        for c0 in range(r0, r0 + b, STRIP):
            tall = r0 + b - c0
            for j in range(STRIP):
                top = j // 8 * 8
                entry = m[c0 + top : r0 + b, c0 + j : c0 + j + 1]
                cols[j, top:tall, :] = jnp.broadcast_to(entry, (tall - top, LANES))
            units = [[] for _ in chunks]
            for base in range(0, STRIP, 8):
                column = [cols[base + j, base:tall, :] for j in range(8)]
                rows = [m[c0 + base : c0 + base + 8, q : q + LANES] for q in chunks]
                for i in range(base):
                    factor = cols[i, base:tall, :]
                    for j in range(8):
                        column[j] = column[j] - factor * cols[i, base + j : base + j + 1, :]
                    for q in range(len(chunks)):
                        rows[q] = rows[q] - factor[:8, :] * units[q][i]
                for j in range(8):
                    scale = lax.rsqrt(column[j][j : j + 1, :])
                    column[j] = column[j] * scale
                    for k in range(j + 1, 8):
                        column[k] = column[k] - column[j] * column[j][k : k + 1, :]
                    if base + 8 < tall:
                        cols[base + j, base:tall, :] = column[j]
                    below = jnp.where(group > j, column[j][:8, :], 0.0)
                    for q in range(len(chunks)):
                        unit = rows[q][j : j + 1, :] * scale
                        units[q].append(unit)
                        if j < 7:
                            rows[q] = rows[q] - below * unit
            for q, start in enumerate(chunks):
                solved[q].append(jnp.concatenate(units[q], axis=0))
                for top in range(STRIP, tall, 8):
                    lower_rows = m[c0 + top : c0 + top + 8, start : start + LANES]
                    for i in range(STRIP):
                        lower_rows = lower_rows - cols[i, top : top + 8, :] * units[q][i]
                    m[c0 + top : c0 + top + 8, start : start + LANES] = lower_rows
        panel = [jnp.concatenate(s, axis=0) for s in solved]
        for q, start in enumerate(chunks):
            if start >= n:
                out[r0 : r0 + b, start - n : start - n + LANES] = panel[q]
        if lower and end < width:
            out[r0 : r0 + b, end - n :] = jnp.zeros((b, width - end), jnp.float32)
        done = r0 + b
        if done < n:
            lo2 = done // LANES * LANES
            block = jnp.concatenate(panel[(lo2 - lo) // LANES :], axis=1)
            high, mid, low = split3(block)
            span = n - lo2
            left = jnp.concatenate([v[:, :span] for v in (high, high, mid, high, mid, low)], axis=0)
            right = jnp.concatenate([high, mid, high, low, mid, high], axis=0)
            update = lax.dot_general(
                left, right, (((0,), (0,)), ((), ())), preferred_element_type=jnp.float32
            )
            m[done:n, lo2:end] = m[done:n, lo2:end] - update[done - lo2 :, :]


def place_of(axes, parts, block, r):
    rows, grp = lax.axis_index(axes[0]), lax.axis_index(axes[1])
    flip = grp & 1
    for bit in range(1, 8):
        flip = flip ^ ((grp >> bit) & 1)
    me = (rows & (parts - 1)) ^ flip
    return pl.multiple_of((me ^ r) * block, LANES)


def pair(x):
    high = x.astype(jnp.bfloat16)
    return high, (x - high.astype(jnp.float32)).astype(jnp.bfloat16)


def dot3(a, b, contract=((1,), (0,))):
    (ah, al), (bh, bl) = a, b
    left = jnp.concatenate([ah, ah, al], axis=contract[0][0])
    right = jnp.concatenate([bh, bl, bh], axis=contract[1][0])
    return lax.dot_general(left, right, (contract, ((), ())), preferred_element_type=jnp.float32)


def start_kernel(axes, parts, kept, z_hbm, s_hbm, keep_ref, send_ref, whole, z_ref, s_ref, sems):
    k = z_ref.shape[1]
    step = min(k, 2 * LANES)
    copies = []
    for i in range(k // step):
        span = pl.ds(i * step, step)
        copies.append((
            pltpu.make_async_copy(z_hbm.at[:, span], z_ref.at[:, span], sems.at[2 * i]),
            pltpu.make_async_copy(s_hbm.at[span, :], s_ref.at[span, :], sems.at[2 * i + 1]),
        ))
        for copy in copies[-1]:
            copy.start()
    image, halves = 0.0, []
    for i, both in enumerate(copies):
        for copy in both:
            copy.wait()
        halves.append(pair(z_ref[:, i * step : (i + 1) * step]))
        image = image + dot3(halves[i], pair(s_ref[i * step : (i + 1) * step, :]))
    turned = pair(image.T)
    for i, z in enumerate(halves):
        whole[:, i * step : (i + 1) * step] = dot3(turned, z)
    block = k // parts
    for i, r in enumerate(kept):
        keep_ref[i] = whole[:, pl.ds(place_of(axes, parts, block, r), block)]
        send_ref[i] = whole[:, pl.ds(place_of(axes, parts, block, r ^ 1), block)]


def first_kernel(s_ref, m_ref, out_ref, cols):
    n = s_ref.shape[1]
    s = s_ref[...]
    m_ref[:, :n] = dot(s.T, s)
    index = lax.broadcasted_iota(jnp.int32, (n, n), 0)
    other = lax.broadcasted_iota(jnp.int32, (n, n), 1)
    m_ref[:, n:] = jnp.where(index == other, 1.0, 0.0)
    eliminate(m_ref, out_ref, n, 0, n // 2, True, cols)


def second_kernel(m_ref, half_ref, z_ref, out_ref, total_ref, m, cols):
    n = m.shape[0]
    m[n // 2 :, :] = m_ref[n // 2 :, :]
    out_ref[: n // 2, :] = half_ref[: n // 2, :]
    eliminate(m, out_ref, n, n // 2, n, True, cols)
    z = z_ref[...]
    total_ref[...] = jnp.sum(z * z, axis=0, keepdims=True)


def shard_kernel(inverse_ref, *refs):
    total = refs[0][...]
    for ref in refs[1:-1]:
        total = total + ref[...]
    refs[-1][...] = dot(inverse_ref[...], total)


def products(axes, parts, numbers, z_ref, refs):
    block = refs[0].shape[2]
    y = jnp.concatenate([ref[i] for ref in refs for i in range(2)], axis=1)
    z = jnp.concatenate(
        [z_ref[:, pl.ds(place_of(axes, parts, block, r), block)] for r in numbers], axis=1
    )
    across = ((1,), (1,))
    return dot(y, y, across), dot3(pair(y), pair(z), across)


def near_kernel(axes, parts, kept, z_ref, near_ref, far_ref, m_ref):
    n = m_ref.shape[0]
    numbers = kept[:2] + [r ^ 1 for r in kept[:2]]
    m_ref[:, :n], m_ref[:, n:] = products(axes, parts, numbers, z_ref, (near_ref, far_ref))


def next_kernel(axes, parts, kept, z_ref, before_ref, near_ref, m_ref):
    n = m_ref.shape[0]
    gram, image = products(axes, parts, kept[2:], z_ref, (near_ref,))
    m_ref[:, :n] = before_ref[:, :n] + gram
    m_ref[:, n:] = before_ref[:, n:] + image


def last_kernel(axes, parts, kept, z_ref, near_ref, far_ref, total_ref, out_hbm, energy_ref, m, solved, out, cols, sems):
    n = near_ref.shape[0]
    gram, image = products(axes, parts, [r ^ 1 for r in kept[2:]], z_ref, (far_ref,))
    m[:, :n] = near_ref[:, :n] + gram
    m[:, n:] = near_ref[:, n:] + image
    half = n // 2
    copies, energy = [], 0.0
    for i in range(2):
        span = pl.ds(i * half, half)
        eliminate(m, solved, n, i * half, (i + 1) * half, False, cols)
        result = solved[i * half : (i + 1) * half, :]
        out[:, i * half : (i + 1) * half] = result.T
        copies.append(pltpu.make_async_copy(out.at[:, span], out_hbm.at[:, span], sems.at[i]))
        copies[i].start()
        energy = energy + jnp.sum(result * result)
    lane = lax.broadcasted_iota(jnp.int32, energy_ref.shape, 2)
    total = jnp.sum(total_ref[...])
    energy_ref[...] = jnp.where(lane == 0, energy, jnp.where(lane == 1, total, 0.0))
    for copy in copies:
        copy.wait()


def share_kernel(energy_ref, out_ref):
    sums = jnp.sum(energy_ref[:, 0, :], axis=0, keepdims=True)
    out_ref[...] = 1.0 - sums[:, 0:1] / sums[:, 1:2]


def call(kernel, outs, scratch, flops, limit, in_hbm=(), out_hbm=()):
    moved = 4 * sum(math.prod(s) for s in outs)

    def run(*args):
        return pl.pallas_call(
            kernel,
            out_shape=[jax.ShapeDtypeStruct(s, jnp.float32) for s in outs],
            in_specs=[HBM if i in in_hbm else VMEM for i in range(len(args))],
            out_specs=[HBM if i in out_hbm else VMEM for i in range(len(outs))],
            scratch_shapes=[
                pltpu.SemaphoreType.DMA((s,)) if isinstance(s, int) else pltpu.VMEM(s, jnp.float32)
                for s in scratch
            ],
            cost_estimate=pl.CostEstimate(flops=flops, bytes_accessed=moved, transcendentals=0),
            compiler_params=pltpu.CompilerParams(vmem_limit_bytes=limit * 2**20),
        )(*args)

    return run


def exchange(x, axis, size, mask):
    return lax.ppermute(x, axis, [(i, i ^ mask) for i in range(size)])


def steps_over(rows_size, grp_size, parts):
    masks = [(1 << i, 0) for i in range(parts.bit_length() - 1, rows_size.bit_length() - 1)]
    masks += [(1, 1 << i) for i in range(grp_size.bit_length() - 1)]

    def pairs(position):
        out = []
        for r in range(rows_size):
            for g in range(grp_size):
                odd = (r ^ bin(g).count("1")) & 1
                row_mask, grp_mask = masks[-1 - position] if odd else masks[position]
                out.append((r * grp_size + g, (r ^ row_mask) * grp_size + (g ^ grp_mask)))
        return out

    return [pairs(i) for i in range(len(masks))]


def local(rows_size, grp_size, factor, start_block):
    own, k = factor.shape
    n = start_block.shape[1]
    parts = 8
    assert rows_size % parts == 0 and k == parts * LANES
    block = k // parts
    half = parts // 2
    panel = (STRIP, PANEL, LANES)
    axes = ("rows", "grp")
    kept = [0] + [2 * i + 1 for i in range(1, half)]
    tie = lax.optimization_barrier
    apart = pltpu.with_memory_space_constraint

    keep, send = call(
        functools.partial(start_kernel, axes, parts, kept),
        [(half, n, block)] * 2, [(n, k), (own, k), (k, n), 2 * (k // min(k, 2 * LANES))], 10**8, 14, (0, 1),
    )(apart(factor, pltpu.HBM), apart(start_block, pltpu.HBM))
    got = exchange(send, "rows", rows_size, 1)
    pieces = [keep[i] + got[i] for i in range(half)]
    pieces[0], start_block = tie((pieces[0], start_block))
    moved = [exchange(pieces[i], "rows", rows_size, kept[i]) for i in range(1, half)]
    first = call(first_kernel, [(n, 2 * n), (n, n)], [panel], 10**10, 8)(start_block)
    first, moved = tie((first, moved))
    total = sum(moved, pieces[0])
    terms = [total]
    for i, pairs in enumerate(steps_over(rows_size, grp_size, parts)):
        total = sum(terms[1:], terms[0])
        other = lax.ppermute(total, axes, pairs)
        if i == 0:
            inverse, energy = call(second_kernel, [(n, n), (1, k)], [(n, 2 * n), panel], 5 * 10**9, 8)(*first, factor)
            inverse, other = tie((inverse, other))
        terms = [total, other]
    (shard,) = call(shard_kernel, [(n, block)], [], 10**8, 4)(inverse, *terms)

    arrived = []
    for r in kept[1:]:
        arrived.append(exchange(shard, "rows", rows_size, r))
    near = jnp.stack([shard, arrived[0]])
    far = exchange(near, "rows", rows_size, 1)
    (begun,) = call(functools.partial(near_kernel, axes, parts, kept), [(n, n + own)], [], 10**9, 8)(factor, near, far)
    begun, arrived[2] = tie((begun, arrived[2]))
    near = jnp.stack(arrived[1:])
    far = exchange(near, "rows", rows_size, 1)
    (begun,) = call(
        functools.partial(next_kernel, axes, parts, kept), [(n, n + own)], [], 10**9, 8
    )(factor, begun, near)
    begun, far = tie((begun, far))
    count = rows_size * grp_size
    compressed, energy = call(
        functools.partial(last_kernel, axes, parts, kept),
        [(own, n), (count, 1, LANES)], [(n, n + own), (n, own), (own, n), panel, 2], 10**10, 12, (), (0,),
    )(factor, begun, far, energy)
    energy = lax.all_to_all(energy, axes, 0, 0, tiled=True)
    (tail_share,) = call(share_kernel, [(1, 1)], [], 10**5, 4)(energy)
    return compressed, tail_share.reshape(())


def solution(mesh):
    def body(factor, start_block):
        return local(mesh.shape["rows"], mesh.shape["grp"], factor, start_block)

    return jax.shard_map(
        body,
        mesh=mesh,
        in_specs=(P(("rows", "grp"), None), P()),
        out_specs=(P(("rows", "grp"), None), P()),
        check_vma=False,
    )
```

profile of v0, /device:TPU:0, one launch (start us, length us, event | category | flops | bytes accessed | tf_op | source)
XLA Modules:
  0.0 64.6 jit_solution(12510819702041908910)
XLA Ops:
  0.6 3.4 %shard_map.41 = (f32[4,256,128]{2,1,0:T(8,128)S(1)}, f32[4,256,128]{2,1,0:T(8,128)S(1)}) custom-call(f32[256,1024]{1,0:T(8,128)} %z_ref.7, f32[1024,256]{1,0:T(8,128)} %s_ref), custom_call_target="tpu_custom_call" | custom-call | flops 100000000 | bytes 1048576 | tf_op jit(solution)/shard_map/pallas_call | solution.py:225
  4.1 0.6 collective-permute-start
  4.6 1.5 %collective-permute-done = f32[4,256,128]{2,1,0:T(8,128)S(1)} collective-permute-done((f32[4,256,128]{2,1,0:T(8,128)S(1)}, f32[4,256,128]{2,1,0:T(8,128)S(1)}, u32[]{:S(2)}, u32[]{:S(2)}) %collective-permute-start) | collective-permute-done | bytes 524320 | tf_op jit(solution)/shard_map/ppermute | solution.py:242
  6.2 3.6 %collective-permute-start.3 = (f32[256,128]{1,0:T(8,128)S(1)}, f32[256,128]{1,0:T(8,128)S(1)}, u32[]{:S(2)}, u32[]{:S(2)}) collective-permute-start(f32[256,128]{1,0:T(8,128)S(1)} %get-tuple-element.44), channel_id=1, source_target_pairs={{0,28},{4,24},{8,20},{12,16},{16,12},{20,8},{24,4},{28,0},{1,29},{... | collective-permute-start | bytes 393224 | tf_op jit(solution)/shard_map/ppermute | solution.py:242
  9.8 0.5 collective-permute-start.2
  10.5 4.2 %shard_map.42 = (f32[256,512]{1,0:T(8,128)S(1)}, f32[256,256]{1,0:T(8,128)S(1)}) custom-call(f32[1024,256]{1,0:T(8,128)S(1)} %copy-done), custom_call_target="tpu_custom_call" | custom-call | flops 10000000000 | bytes 786432 | tf_op jit(solution)/shard_map/pallas_call | solution.py:225
  14.6 2.0 %collective-permute-done.2 = f32[256,128]{1,0:T(8,128)S(1)} collective-permute-done((f32[256,128]{1,0:T(8,128)S(1)}, f32[256,128]{1,0:T(8,128)S(1)}, u32[]{:S(2)}, u32[]{:S(2)}) %collective-permute-start.2) | collective-permute-done | bytes 131104 | tf_op jit(solution)/shard_map/ppermute | solution.py:242
  17.0 1.5 %collective-permute-start.4 = (f32[256,128]{1,0:T(8,128)S(1)}, f32[256,128]{1,0:T(8,128)S(1)}, u32[]{:S(2)}, u32[]{:S(2)}) collective-permute-start(f32[256,128]{1,0:T(8,128)S(1)} %add_add_fusion), channel_id=1, source_target_pairs={{0,5},{1,7},{2,4},{3,6},{4,2},{5,0},{6,3},{7,1},{8,13},{9,15},{10,... | collective-permute-start | bytes 393224 | tf_op jit(solution)/shard_map/ppermute | solution.py:288
  18.5 2.8 %shard_map.43 = (f32[256,256]{1,0:T(8,128)S(1)}, f32[1,1024]{1,0:T(1,128)S(1)}) custom-call(f32[256,512]{1,0:T(8,128)S(1)} %get-tuple-element.28.m_ref, f32[256,256]{1,0:T(8,128)S(1)} %get-tuple-element.29.half_ref, f32[256,1024]{1,0:T(8,128)S(1)} %copy-done.1), custom_call_target="tpu_custom_call" | custom-call | flops 5000000000 | bytes 266240 | tf_op jit(solution)/shard_map/pallas_call | solution.py:225
  21.7 3.6 %collective-permute-start.5 = (f32[256,128]{1,0:T(8,128)S(1)}, f32[256,128]{1,0:T(8,128)S(1)}, u32[]{:S(2)}, u32[]{:S(2)}) collective-permute-start(f32[256,128]{1,0:T(8,128)S(1)} %add.47.refs_0_), channel_id=1, source_target_pairs={{0,6},{1,4},{2,7},{3,5},{4,1},{5,3},{6,0},{7,2},{8,14},{9,12},{10,... | collective-permute-start | bytes 393224 | tf_op jit(solution)/shard_map/ppermute | solution.py:288
  25.3 3.2 %collective-permute-done.5.refs_1_ = f32[256,128]{1,0:T(8,128)S(1)} collective-permute-done((f32[256,128]{1,0:T(8,128)S(1)}, f32[256,128]{1,0:T(8,128)S(1)}, u32[]{:S(2)}, u32[]{:S(2)}) %collective-permute-start.5) | collective-permute-done | bytes 131104 | tf_op jit(solution)/shard_map/ppermute | solution.py:288
  28.9 1.9 %collective-permute-start.6 = (f32[256,128]{1,0:T(8,128)S(1)}, f32[256,128]{1,0:T(8,128)S(1)}, u32[]{:S(2)}, u32[]{:S(2)}) collective-permute-start(f32[256,128]{1,0:T(8,128)S(1)} %shard_map.44), channel_id=1, source_target_pairs={{0,12},{4,8},{8,4},{12,0},{16,28},{20,24},{24,20},{28,16},{1,13},{... | collective-permute-start | bytes 393224 | tf_op jit(solution)/shard_map/ppermute | solution.py:242
  30.7 3.2 %collective-permute-done.6 = f32[256,128]{1,0:T(8,128)S(1)} collective-permute-done((f32[256,128]{1,0:T(8,128)S(1)}, f32[256,128]{1,0:T(8,128)S(1)}, u32[]{:S(2)}, u32[]{:S(2)}) %collective-permute-start.6) | collective-permute-done | bytes 131104 | tf_op jit(solution)/shard_map/ppermute | solution.py:242
  34.0 0.7 %collective-permute-start.7 = (f32[2,256,128]{2,1,0:T(8,128)S(1)}, f32[2,256,128]{2,1,0:T(8,128)S(1)}, u32[]{:S(2)}, u32[]{:S(2)}) collective-permute-start(f32[2,256,128]{2,1,0:T(8,128)S(1)} %pad_maximum_fusion.near_ref), channel_id=1, source_target_pairs={{0,4},{4,0},{8,12},{12,8},{16,20},{20,16},{24,28},{28,24},{1,5},{5... | collective-permute-start | bytes 786440 | tf_op jit(solution)/shard_map/ppermute | solution.py:242
  34.7 1.2 %collective-permute-start.8 = (f32[256,128]{1,0:T(8,128)S(1)}, f32[256,128]{1,0:T(8,128)S(1)}, u32[]{:S(2)}, u32[]{:S(2)}) collective-permute-start(f32[256,128]{1,0:T(8,128)S(1)} %shard_map.44), channel_id=1, source_target_pairs={{0,28},{4,24},{8,20},{12,16},{16,12},{20,8},{24,4},{28,0},{1,29},{... | collective-permute-start | bytes 393224 | tf_op jit(solution)/shard_map/ppermute | solution.py:242
  35.9 1.4 %collective-permute-start.9 = (f32[256,128]{1,0:T(8,128)S(1)}, f32[256,128]{1,0:T(8,128)S(1)}, u32[]{:S(2)}, u32[]{:S(2)}) collective-permute-start(f32[256,128]{1,0:T(8,128)S(1)} %shard_map.44), channel_id=1, source_target_pairs={{0,20},{4,16},{8,28},{12,24},{16,4},{20,0},{24,12},{28,8},{1,21},{... | collective-permute-start | bytes 393224 | tf_op jit(solution)/shard_map/ppermute | solution.py:242
  37.3 0.9 %shard_map.45.before_ref = f32[256,512]{1,0:T(8,128)S(1)} custom-call(f32[256,1024]{1,0:T(8,128)S(1)} %copy-done.1, f32[2,256,128]{2,1,0:T(8,128)S(1)} %pad_maximum_fusion.near_ref, f32[2,256,128]{2,1,0:T(8,128)S(1)} %collective-permute-done.7.far_ref), custom_call_target="tpu_custom_call" | custom-call | flops 1000000000 | bytes 524288 | tf_op jit(solution)/shard_map/pallas_call | solution.py:225
  38.2 3.0 %collective-permute-done.8 = f32[256,128]{1,0:T(8,128)S(1)} collective-permute-done((f32[256,128]{1,0:T(8,128)S(1)}, f32[256,128]{1,0:T(8,128)S(1)}, u32[]{:S(2)}, u32[]{:S(2)}) %collective-permute-start.8) | collective-permute-done | bytes 131104 | tf_op jit(solution)/shard_map/ppermute | solution.py:242
  41.2 2.9 %collective-permute-done.9 = f32[256,128]{1,0:T(8,128)S(1)} collective-permute-done((f32[256,128]{1,0:T(8,128)S(1)}, f32[256,128]{1,0:T(8,128)S(1)}, u32[]{:S(2)}, u32[]{:S(2)}) %collective-permute-start.9) | collective-permute-done | bytes 131104 | tf_op jit(solution)/shard_map/ppermute | solution.py:242
  44.3 0.6 shard_map.46.near_ref
  44.9 0.9 %collective-permute-done.10.far_ref = f32[2,256,128]{2,1,0:T(8,128)S(1)} collective-permute-done((f32[2,256,128]{2,1,0:T(8,128)S(1)}, f32[2,256,128]{2,1,0:T(8,128)S(1)}, u32[]{:S(2)}, u32[]{:S(2)}) %collective-permute-start.10) | collective-permute-done | bytes 262176 | tf_op jit(solution)/shard_map/ppermute | solution.py:242
  45.8 7.1 %shard_map.47 = (f32[256,256]{1,0:T(8,128)}, f32[32,1,128]{2,1,0:T(1,128)S(1)}) custom-call(f32[256,1024]{1,0:T(8,128)S(1)} %copy-done.1, f32[256,512]{1,0:T(8,128)S(1)} %shard_map.46.near_ref, f32[2,256,128]{2,1,0:T(8,128)S(1)} %collective-permute-done.10.far_ref, f32[1,1024]{1,0:T(1,128)S(1)} %get-tuple-element.41.total_ref), custom_call_target="tpu_custom_call" | custom-call | flops 10000000000 | bytes 278528 | tf_op jit(solution)/shard_map/pallas_call | solution.py:225
  52.8 11.1 %all_to_all.5.energy_ref = f32[32,1,128]{2,1,0:T(1,128)S(1)} all-to-all(f32[32,1,128]{2,1,0:T(1,128)S(1)} %get-tuple-element.43), channel_id=1, replica_groups=mesh['rows'=8,'grp'=4] {'rows','grp'}, dimensions={0} | all-to-all | bytes 32768 | tf_op jit(solution)/shard_map/all_to_all | solution.py:313
  64.0 0.6 shard_map.48
  (16 shorter events, 1.5 us)
Async XLA Ops:
  4.0 6.4 %copy-start = (f32[1024,256]{1,0:T(8,128)S(1)}, f32[1024,256]{1,0:T(8,128)}, u32[]{:S(2)}) copy-start(f32[1024,256]{1,0:T(8,128)} %s_ref) | copy-start | bytes 3145732
  4.1 2.1 %collective-permute-start = (f32[4,256,128]{2,1,0:T(8,128)S(1)}, f32[4,256,128]{2,1,0:T(8,128)S(1)}, u32[]{:S(2)}, u32[]{:S(2)}) collective-permute-start(f32[4,256,128]{2,1,0:T(8,128)S(1)} %get-tuple-element.24), channel_id=1, source_target_pairs={{0,4},{4,0},{8,12},{12,8},{16,20},{20,16},{24,28},{28,24},{1,5},{5... | collective-permute-start | bytes 1572872 | tf_op jit(solution)/shard_map/ppermute | solution.py:242
  6.2 8.4 %collective-permute-start.3 = (f32[256,128]{1,0:T(8,128)S(1)}, f32[256,128]{1,0:T(8,128)S(1)}, u32[]{:S(2)}, u32[]{:S(2)}) collective-permute-start(f32[256,128]{1,0:T(8,128)S(1)} %get-tuple-element.44), channel_id=1, source_target_pairs={{0,28},{4,24},{8,20},{12,16},{16,12},{20,8},{24,4},{28,0},{1,29},{... | collective-permute-start | bytes 393224 | tf_op jit(solution)/shard_map/ppermute | solution.py:242
  9.8 6.8 %collective-permute-start.2 = (f32[256,128]{1,0:T(8,128)S(1)}, f32[256,128]{1,0:T(8,128)S(1)}, u32[]{:S(2)}, u32[]{:S(2)}) collective-permute-start(f32[256,128]{1,0:T(8,128)S(1)} %get-tuple-element.45), channel_id=1, source_target_pairs={{0,20},{4,16},{8,28},{12,24},{16,4},{20,0},{24,12},{28,8},{1,21},{... | collective-permute-start | bytes 393224 | tf_op jit(solution)/shard_map/ppermute | solution.py:242
  10.3 8.2 %copy-start.1 = (f32[256,1024]{1,0:T(8,128)S(1)}, f32[256,1024]{1,0:T(8,128)}, u32[]{:S(2)}) copy-start(f32[256,1024]{1,0:T(8,128)} %z_ref.7) | copy-start | bytes 3145732
  10.3 6.6 %collective-permute-start.1 = (f32[256,128]{1,0:T(8,128)S(1)}, f32[256,128]{1,0:T(8,128)S(1)}, u32[]{:S(2)}, u32[]{:S(2)}) collective-permute-start(f32[256,128]{1,0:T(8,128)S(1)} %get-tuple-element.46), channel_id=1, source_target_pairs={{0,12},{4,8},{8,4},{12,0},{16,28},{20,24},{24,20},{28,16},{1,13},{... | collective-permute-start | bytes 393224 | tf_op jit(solution)/shard_map/ppermute | solution.py:242
  17.0 4.7 %collective-permute-start.4 = (f32[256,128]{1,0:T(8,128)S(1)}, f32[256,128]{1,0:T(8,128)S(1)}, u32[]{:S(2)}, u32[]{:S(2)}) collective-permute-start(f32[256,128]{1,0:T(8,128)S(1)} %add_add_fusion), channel_id=1, source_target_pairs={{0,5},{1,7},{2,4},{3,6},{4,2},{5,0},{6,3},{7,1},{8,13},{9,15},{10,... | collective-permute-start | bytes 393224 | tf_op jit(solution)/shard_map/ppermute | solution.py:288
  21.7 6.8 %collective-permute-start.5 = (f32[256,128]{1,0:T(8,128)S(1)}, f32[256,128]{1,0:T(8,128)S(1)}, u32[]{:S(2)}, u32[]{:S(2)}) collective-permute-start(f32[256,128]{1,0:T(8,128)S(1)} %add.47.refs_0_), channel_id=1, source_target_pairs={{0,6},{1,4},{2,7},{3,5},{4,1},{5,3},{6,0},{7,2},{8,14},{9,12},{10,... | collective-permute-start | bytes 393224 | tf_op jit(solution)/shard_map/ppermute | solution.py:288
  28.9 5.1 %collective-permute-start.6 = (f32[256,128]{1,0:T(8,128)S(1)}, f32[256,128]{1,0:T(8,128)S(1)}, u32[]{:S(2)}, u32[]{:S(2)}) collective-permute-start(f32[256,128]{1,0:T(8,128)S(1)} %shard_map.44), channel_id=1, source_target_pairs={{0,12},{4,8},{8,4},{12,0},{16,28},{20,24},{24,20},{28,16},{1,13},{... | collective-permute-start | bytes 393224 | tf_op jit(solution)/shard_map/ppermute | solution.py:242
  34.0 3.3 %collective-permute-start.7 = (f32[2,256,128]{2,1,0:T(8,128)S(1)}, f32[2,256,128]{2,1,0:T(8,128)S(1)}, u32[]{:S(2)}, u32[]{:S(2)}) collective-permute-start(f32[2,256,128]{2,1,0:T(8,128)S(1)} %pad_maximum_fusion.near_ref), channel_id=1, source_target_pairs={{0,4},{4,0},{8,12},{12,8},{16,20},{20,16},{24,28},{28,24},{1,5},{5... | collective-permute-start | bytes 786440 | tf_op jit(solution)/shard_map/ppermute | solution.py:242
  34.7 6.5 %collective-permute-start.8 = (f32[256,128]{1,0:T(8,128)S(1)}, f32[256,128]{1,0:T(8,128)S(1)}, u32[]{:S(2)}, u32[]{:S(2)}) collective-permute-start(f32[256,128]{1,0:T(8,128)S(1)} %shard_map.44), channel_id=1, source_target_pairs={{0,28},{4,24},{8,20},{12,16},{16,12},{20,8},{24,4},{28,0},{1,29},{... | collective-permute-start | bytes 393224 | tf_op jit(solution)/shard_map/ppermute | solution.py:242
  35.9 8.3 %collective-permute-start.9 = (f32[256,128]{1,0:T(8,128)S(1)}, f32[256,128]{1,0:T(8,128)S(1)}, u32[]{:S(2)}, u32[]{:S(2)}) collective-permute-start(f32[256,128]{1,0:T(8,128)S(1)} %shard_map.44), channel_id=1, source_target_pairs={{0,20},{4,16},{8,28},{12,24},{16,4},{20,0},{24,12},{28,8},{1,21},{... | collective-permute-start | bytes 393224 | tf_op jit(solution)/shard_map/ppermute | solution.py:242
  44.2 1.6 %collective-permute-start.10 = (f32[2,256,128]{2,1,0:T(8,128)S(1)}, f32[2,256,128]{2,1,0:T(8,128)S(1)}, u32[]{:S(2)}, u32[]{:S(2)}) collective-permute-start(f32[2,256,128]{2,1,0:T(8,128)S(1)} %pad_maximum_fusion.1.near_ref), channel_id=1, source_target_pairs={{0,4},{4,0},{8,12},{12,8},{16,20},{20,16},{24,28},{28,24},{1,5},{5... | collective-permute-start | bytes 786440 | tf_op jit(solution)/shard_map/ppermute | solution.py:242
where the time goes:
time: 64.8 us; the launch traced here: 64.6 us
  Pallas kernels  19.8 us (31%)
  waiting for transfers between devices  17.4 us (27%)
  starting transfers between devices  15.3 us (24%)
  blocking collectives  11.1 us (17%)
  between operations  0.72 us (1%)
    pallas_call x8, Pallas kernels, run(): pl.pallas_call(kernel, out_shape=[jax.ShapeDtypeStruct(s, jnp.float32) fo...  19.8 us
    ppermute x9, waiting for transfers between devices, exchange(): return lax.ppermute(x, axis, [(i, i ^ mask) for i in range(size)])  13.9 us
    all_to_all x1, blocking collectives, local(): energy = lax.all_to_all(energy, axes, 0, 0, tiled=True)  11.1 us
    ppermute x9, starting transfers between devices, exchange(): return lax.ppermute(x, axis, [(i, i ^ mask) for i in range(size)])  10.2 us
    ppermute x2, starting transfers between devices, local(): other = lax.ppermute(total, axes, pairs)  5.12 us
    ppermute x2, waiting for transfers between devices, local(): other = lax.ppermute(total, axes, pairs)  3.55 us
  transfers between devices with their start and end apart: 11, of which 9 were waited for; matrix products, arithmetic and copies ran while one was open for 0% of the time, Pallas kernels for 13%

commit v1 on v0

--- a/solution.py
+++ b/solution.py
@@ -191,34 +191,38 @@
     m_ref[:, n:] = before_ref[:, n:] + image
 
 
-def last_kernel(axes, parts, kept, z_ref, near_ref, far_ref, total_ref, out_hbm, energy_ref, m, solved, out, cols, sems):
+def last_kernel(axes, parts, kept, z_ref, near_ref, far_ref, total_ref, out_hbm, energy_ref, rest_ref, m, solved, out, cols, sems):
     n = near_ref.shape[0]
     gram, image = products(axes, parts, [r ^ 1 for r in kept[2:]], z_ref, (far_ref,))
     m[:, :n] = near_ref[:, :n] + gram
     m[:, n:] = near_ref[:, n:] + image
     half = n // 2
-    copies, energy = [], 0.0
-    for i in range(2):
-        span = pl.ds(i * half, half)
-        eliminate(m, solved, n, i * half, (i + 1) * half, False, cols)
-        result = solved[i * half : (i + 1) * half, :]
-        out[:, i * half : (i + 1) * half] = result.T
-        copies.append(pltpu.make_async_copy(out.at[:, span], out_hbm.at[:, span], sems.at[i]))
-        copies[i].start()
-        energy = energy + jnp.sum(result * result)
+    eliminate(m, solved, n, 0, half, False, cols)
+    first = solved[:half, :]
+    out[...] = first.T
+    copy = pltpu.make_async_copy(out, out_hbm.at[:, pl.ds(0, half)], sems.at[0])
+    copy.start()
+    eliminate(m, solved, n, half, n, False, cols)
+    second = solved[half:, :]
+    rest_ref[...] = second
+    energy = jnp.sum(first * first) + jnp.sum(second * second)
     lane = lax.broadcasted_iota(jnp.int32, energy_ref.shape, 2)
     total = jnp.sum(total_ref[...])
     energy_ref[...] = jnp.where(lane == 0, energy, jnp.where(lane == 1, total, 0.0))
-    for copy in copies:
-        copy.wait()
-
-
-def share_kernel(energy_ref, out_ref):
+    copy.wait()
+
+
+def share_kernel(energy_ref, rest_ref, begun_hbm, out_hbm, share_ref, turned, sems):
+    half = rest_ref.shape[0]
+    turned[...] = rest_ref[...].T
+    copy = pltpu.make_async_copy(turned, out_hbm.at[:, pl.ds(half, half)], sems.at[0])
+    copy.start()
     sums = jnp.sum(energy_ref[:, 0, :], axis=0, keepdims=True)
-    out_ref[...] = 1.0 - sums[:, 0:1] / sums[:, 1:2]
-
-
-def call(kernel, outs, scratch, flops, limit, in_hbm=(), out_hbm=()):
+    share_ref[...] = 1.0 - sums[:, 0:1] / sums[:, 1:2]
+    copy.wait()
+
+
+def call(kernel, outs, scratch, flops, limit, in_hbm=(), out_hbm=(), aliases=()):
     moved = 4 * sum(math.prod(s) for s in outs)
 
     def run(*args):
@@ -233,6 +237,7 @@
             ],
             cost_estimate=pl.CostEstimate(flops=flops, bytes_accessed=moved, transcendentals=0),
             compiler_params=pltpu.CompilerParams(vmem_limit_bytes=limit * 2**20),
+            input_output_aliases=dict(aliases),
         )(*args)
 
     return run
@@ -306,12 +311,14 @@
     )(factor, begun, near)
     begun, far = tie((begun, far))
     count = rows_size * grp_size
-    compressed, energy = call(
+    compressed, energy, rest = call(
         functools.partial(last_kernel, axes, parts, kept),
-        [(own, n), (count, 1, LANES)], [(n, n + own), (n, own), (own, n), panel, 2], 10**10, 12, (), (0,),
+        [(own, n), (count, 1, LANES), (n // 2, own)], [(n, n + own), (n, own), (own, n // 2), panel, 1], 10**10, 12, (), (0,),
     )(factor, begun, far, energy)
     energy = lax.all_to_all(energy, axes, 0, 0, tiled=True)
-    (tail_share,) = call(share_kernel, [(1, 1)], [], 10**5, 4)(energy)
+    compressed, tail_share = call(
+        share_kernel, [(own, n), (1, 1)], [(own, n // 2), 1], 10**5, 4, (2,), (0,), ((2, 0),)
+    )(energy, rest, compressed)
     return compressed, tail_share.reshape(())
 
 

time: 64.8 us -> 65.4 us (level)
  Pallas kernels: 19.8 us -> 20.5 us
    pallas_call x8, Pallas kernels: 19.8 us -> 20.5 us  [run(): pl.pallas_call(kernel, out_shape=[jax.ShapeDtypeStruct(s, jnp.float32) fo...]
where the time goes in v1:
time: 65.4 us; the launch traced here: 65.3 us
  Pallas kernels  20.5 us (31%)
  waiting for transfers between devices  17.4 us (27%)
  starting transfers between devices  15.3 us (23%)
  blocking collectives  11.1 us (17%)
  between operations  0.73 us (1%)
    pallas_call x8, Pallas kernels, run(): pl.pallas_call(kernel, out_shape=[jax.ShapeDtypeStruct(s, jnp.float32) fo...  20.5 us
    ppermute x9, waiting for transfers between devices, exchange(): return lax.ppermute(x, axis, [(i, i ^ mask) for i in range(size)])  13.9 us
    all_to_all x1, blocking collectives, local(): energy = lax.all_to_all(energy, axes, 0, 0, tiled=True)  11.1 us
    ppermute x9, starting transfers between devices, exchange(): return lax.ppermute(x, axis, [(i, i ^ mask) for i in range(size)])  10.2 us
    ppermute x2, starting transfers between devices, local(): other = lax.ppermute(total, axes, pairs)  5.12 us
    ppermute x2, waiting for transfers between devices, local(): other = lax.ppermute(total, axes, pairs)  3.55 us
  transfers between devices with their start and end apart: 11, of which 9 were waited for; matrix products, arithmetic and copies ran while one was open for 0% of the time, Pallas kernels for 13%

profile of v1, /device:TPU:0, one launch (start us, length us, event | category | flops | bytes accessed | tf_op | source)
XLA Modules:
  0.0 65.3 jit_solution(4708940647181461970)
XLA Ops:
  0.6 3.4 %shard_map.41 = (f32[4,256,128]{2,1,0:T(8,128)S(1)}, f32[4,256,128]{2,1,0:T(8,128)S(1)}) custom-call(f32[256,1024]{1,0:T(8,128)} %z_ref.7, f32[1024,256]{1,0:T(8,128)} %s_ref), custom_call_target="tpu_custom_call" | custom-call | flops 100000000 | bytes 1048576 | tf_op jit(solution)/shard_map/pallas_call | solution.py:229
  4.1 0.6 collective-permute-start
  4.6 1.5 %collective-permute-done = f32[4,256,128]{2,1,0:T(8,128)S(1)} collective-permute-done((f32[4,256,128]{2,1,0:T(8,128)S(1)}, f32[4,256,128]{2,1,0:T(8,128)S(1)}, u32[]{:S(2)}, u32[]{:S(2)}) %collective-permute-start) | collective-permute-done | bytes 524320 | tf_op jit(solution)/shard_map/ppermute | solution.py:247
  6.2 3.6 %collective-permute-start.3 = (f32[256,128]{1,0:T(8,128)S(1)}, f32[256,128]{1,0:T(8,128)S(1)}, u32[]{:S(2)}, u32[]{:S(2)}) collective-permute-start(f32[256,128]{1,0:T(8,128)S(1)} %get-tuple-element.50), channel_id=1, source_target_pairs={{0,28},{4,24},{8,20},{12,16},{16,12},{20,8},{24,4},{28,0},{1,29},{... | collective-permute-start | bytes 393224 | tf_op jit(solution)/shard_map/ppermute | solution.py:247
  9.8 0.5 collective-permute-start.2
  10.5 4.2 %shard_map.42 = (f32[256,512]{1,0:T(8,128)S(1)}, f32[256,256]{1,0:T(8,128)S(1)}) custom-call(f32[1024,256]{1,0:T(8,128)S(1)} %copy-done), custom_call_target="tpu_custom_call" | custom-call | flops 10000000000 | bytes 786432 | tf_op jit(solution)/shard_map/pallas_call | solution.py:229
  14.6 2.0 %collective-permute-done.2 = f32[256,128]{1,0:T(8,128)S(1)} collective-permute-done((f32[256,128]{1,0:T(8,128)S(1)}, f32[256,128]{1,0:T(8,128)S(1)}, u32[]{:S(2)}, u32[]{:S(2)}) %collective-permute-start.2) | collective-permute-done | bytes 131104 | tf_op jit(solution)/shard_map/ppermute | solution.py:247
  17.0 1.5 %collective-permute-start.4 = (f32[256,128]{1,0:T(8,128)S(1)}, f32[256,128]{1,0:T(8,128)S(1)}, u32[]{:S(2)}, u32[]{:S(2)}) collective-permute-start(f32[256,128]{1,0:T(8,128)S(1)} %add_add_fusion), channel_id=1, source_target_pairs={{0,5},{1,7},{2,4},{3,6},{4,2},{5,0},{6,3},{7,1},{8,13},{9,15},{10,... | collective-permute-start | bytes 393224 | tf_op jit(solution)/shard_map/ppermute | solution.py:293
  18.5 2.8 %shard_map.43 = (f32[256,256]{1,0:T(8,128)S(1)}, f32[1,1024]{1,0:T(1,128)S(1)}) custom-call(f32[256,512]{1,0:T(8,128)S(1)} %get-tuple-element.31.m_ref, f32[256,256]{1,0:T(8,128)S(1)} %get-tuple-element.32.half_ref, f32[256,1024]{1,0:T(8,128)S(1)} %copy-done.1), custom_call_target="tpu_custom_call" | custom-call | flops 5000000000 | bytes 266240 | tf_op jit(solution)/shard_map/pallas_call | solution.py:229
  21.7 3.6 %collective-permute-start.5 = (f32[256,128]{1,0:T(8,128)S(1)}, f32[256,128]{1,0:T(8,128)S(1)}, u32[]{:S(2)}, u32[]{:S(2)}) collective-permute-start(f32[256,128]{1,0:T(8,128)S(1)} %add.47.refs_0_), channel_id=1, source_target_pairs={{0,6},{1,4},{2,7},{3,5},{4,1},{5,3},{6,0},{7,2},{8,14},{9,12},{10,... | collective-permute-start | bytes 393224 | tf_op jit(solution)/shard_map/ppermute | solution.py:293
  25.3 3.2 %collective-permute-done.5.refs_1_ = f32[256,128]{1,0:T(8,128)S(1)} collective-permute-done((f32[256,128]{1,0:T(8,128)S(1)}, f32[256,128]{1,0:T(8,128)S(1)}, u32[]{:S(2)}, u32[]{:S(2)}) %collective-permute-start.5) | collective-permute-done | bytes 131104 | tf_op jit(solution)/shard_map/ppermute | solution.py:293
  28.9 1.9 %collective-permute-start.6 = (f32[256,128]{1,0:T(8,128)S(1)}, f32[256,128]{1,0:T(8,128)S(1)}, u32[]{:S(2)}, u32[]{:S(2)}) collective-permute-start(f32[256,128]{1,0:T(8,128)S(1)} %shard_map.44), channel_id=1, source_target_pairs={{0,12},{4,8},{8,4},{12,0},{16,28},{20,24},{24,20},{28,16},{1,13},{... | collective-permute-start | bytes 393224 | tf_op jit(solution)/shard_map/ppermute | solution.py:247
  30.7 3.2 %collective-permute-done.6 = f32[256,128]{1,0:T(8,128)S(1)} collective-permute-done((f32[256,128]{1,0:T(8,128)S(1)}, f32[256,128]{1,0:T(8,128)S(1)}, u32[]{:S(2)}, u32[]{:S(2)}) %collective-permute-start.6) | collective-permute-done | bytes 131104 | tf_op jit(solution)/shard_map/ppermute | solution.py:247
  34.0 0.7 %collective-permute-start.7 = (f32[2,256,128]{2,1,0:T(8,128)S(1)}, f32[2,256,128]{2,1,0:T(8,128)S(1)}, u32[]{:S(2)}, u32[]{:S(2)}) collective-permute-start(f32[2,256,128]{2,1,0:T(8,128)S(1)} %pad_maximum_fusion.near_ref), channel_id=1, source_target_pairs={{0,4},{4,0},{8,12},{12,8},{16,20},{20,16},{24,28},{28,24},{1,5},{5... | collective-permute-start | bytes 786440 | tf_op jit(solution)/shard_map/ppermute | solution.py:247
  34.7 1.2 %collective-permute-start.8 = (f32[256,128]{1,0:T(8,128)S(1)}, f32[256,128]{1,0:T(8,128)S(1)}, u32[]{:S(2)}, u32[]{:S(2)}) collective-permute-start(f32[256,128]{1,0:T(8,128)S(1)} %shard_map.44), channel_id=1, source_target_pairs={{0,28},{4,24},{8,20},{12,16},{16,12},{20,8},{24,4},{28,0},{1,29},{... | collective-permute-start | bytes 393224 | tf_op jit(solution)/shard_map/ppermute | solution.py:247
  35.9 1.4 %collective-permute-start.9 = (f32[256,128]{1,0:T(8,128)S(1)}, f32[256,128]{1,0:T(8,128)S(1)}, u32[]{:S(2)}, u32[]{:S(2)}) collective-permute-start(f32[256,128]{1,0:T(8,128)S(1)} %shard_map.44), channel_id=1, source_target_pairs={{0,20},{4,16},{8,28},{12,24},{16,4},{20,0},{24,12},{28,8},{1,21},{... | collective-permute-start | bytes 393224 | tf_op jit(solution)/shard_map/ppermute | solution.py:247
  37.3 0.9 %shard_map.45.before_ref = f32[256,512]{1,0:T(8,128)S(1)} custom-call(f32[256,1024]{1,0:T(8,128)S(1)} %copy-done.1, f32[2,256,128]{2,1,0:T(8,128)S(1)} %pad_maximum_fusion.near_ref, f32[2,256,128]{2,1,0:T(8,128)S(1)} %collective-permute-done.7.far_ref), custom_call_target="tpu_custom_call" | custom-call | flops 1000000000 | bytes 524288 | tf_op jit(solution)/shard_map/pallas_call | solution.py:229
  38.2 3.0 %collective-permute-done.8 = f32[256,128]{1,0:T(8,128)S(1)} collective-permute-done((f32[256,128]{1,0:T(8,128)S(1)}, f32[256,128]{1,0:T(8,128)S(1)}, u32[]{:S(2)}, u32[]{:S(2)}) %collective-permute-start.8) | collective-permute-done | bytes 131104 | tf_op jit(solution)/shard_map/ppermute | solution.py:247
  41.2 2.9 %collective-permute-done.9 = f32[256,128]{1,0:T(8,128)S(1)} collective-permute-done((f32[256,128]{1,0:T(8,128)S(1)}, f32[256,128]{1,0:T(8,128)S(1)}, u32[]{:S(2)}, u32[]{:S(2)}) %collective-permute-start.9) | collective-permute-done | bytes 131104 | tf_op jit(solution)/shard_map/ppermute | solution.py:247
  44.3 0.6 shard_map.46.near_ref
  44.9 0.9 %collective-permute-done.10.far_ref = f32[2,256,128]{2,1,0:T(8,128)S(1)} collective-permute-done((f32[2,256,128]{2,1,0:T(8,128)S(1)}, f32[2,256,128]{2,1,0:T(8,128)S(1)}, u32[]{:S(2)}, u32[]{:S(2)}) %collective-permute-start.10) | collective-permute-done | bytes 262176 | tf_op jit(solution)/shard_map/ppermute | solution.py:247
  45.8 7.0 %shard_map.47 = (f32[256,256]{1,0:T(8,128)}, f32[32,1,128]{2,1,0:T(1,128)S(1)}, f32[128,256]{1,0:T(8,128)S(1)}) custom-call(f32[256,1024]{1,0:T(8,128)S(1)} %copy-done.1, f32[256,512]{1,0:T(8,128)S(1)} %shard_map.46.near_ref, f32[2,256,128]{2,1,0:T(8,128)S(1)} %collective-permute-done.10.far_ref, f32[1,1024]{1,0:T(1,128)S(1)} %get-tuple-element.44.total_ref), custom_call_target="tpu_custom_call" | custom-call | flops 10000000000 | bytes 409600 | tf_op jit(solution)/shard_map/pallas_call | solution.py:229
  52.8 11.1 %all_to_all.5.energy_ref = f32[32,1,128]{2,1,0:T(1,128)S(1)} all-to-all(f32[32,1,128]{2,1,0:T(1,128)S(1)} %get-tuple-element.45), channel_id=1, replica_groups=mesh['rows'=8,'grp'=4] {'rows','grp'}, dimensions={0} | all-to-all | bytes 32768 | tf_op jit(solution)/shard_map/all_to_all | solution.py:318
  64.0 1.3 %shard_map.48 = (f32[256,256]{1,0:T(8,128)}, f32[1,1]{1,0:T(1,128)}) custom-call(f32[32,1,128]{2,1,0:T(1,128)S(1)} %all_to_all.5.energy_ref, f32[128,256]{1,0:T(8,128)S(1)} %get-tuple-element.46.rest_ref, f32[256,256]{1,0:T(8,128)} %get-tuple-element.47.begun_hbm), custom_call_target="tpu_custom_call", output_to_operand_aliasing={{0}: (2, {})} | custom-call | flops 100000 | bytes 262148 | tf_op jit(solution)/shard_map/pallas_call | solution.py:229
  (16 shorter events, 1.5 us)
Async XLA Ops:
  4.0 6.4 %copy-start = (f32[1024,256]{1,0:T(8,128)S(1)}, f32[1024,256]{1,0:T(8,128)}, u32[]{:S(2)}) copy-start(f32[1024,256]{1,0:T(8,128)} %s_ref) | copy-start | bytes 3145732
  4.1 2.1 %collective-permute-start = (f32[4,256,128]{2,1,0:T(8,128)S(1)}, f32[4,256,128]{2,1,0:T(8,128)S(1)}, u32[]{:S(2)}, u32[]{:S(2)}) collective-permute-start(f32[4,256,128]{2,1,0:T(8,128)S(1)} %get-tuple-element.27), channel_id=1, source_target_pairs={{0,4},{4,0},{8,12},{12,8},{16,20},{20,16},{24,28},{28,24},{1,5},{5... | collective-permute-start | bytes 1572872 | tf_op jit(solution)/shard_map/ppermute | solution.py:247
  6.2 8.4 %collective-permute-start.3 = (f32[256,128]{1,0:T(8,128)S(1)}, f32[256,128]{1,0:T(8,128)S(1)}, u32[]{:S(2)}, u32[]{:S(2)}) collective-permute-start(f32[256,128]{1,0:T(8,128)S(1)} %get-tuple-element.50), channel_id=1, source_target_pairs={{0,28},{4,24},{8,20},{12,16},{16,12},{20,8},{24,4},{28,0},{1,29},{... | collective-permute-start | bytes 393224 | tf_op jit(solution)/shard_map/ppermute | solution.py:247
  9.8 6.8 %collective-permute-start.2 = (f32[256,128]{1,0:T(8,128)S(1)}, f32[256,128]{1,0:T(8,128)S(1)}, u32[]{:S(2)}, u32[]{:S(2)}) collective-permute-start(f32[256,128]{1,0:T(8,128)S(1)} %get-tuple-element.51), channel_id=1, source_target_pairs={{0,20},{4,16},{8,28},{12,24},{16,4},{20,0},{24,12},{28,8},{1,21},{... | collective-permute-start | bytes 393224 | tf_op jit(solution)/shard_map/ppermute | solution.py:247
  10.3 8.2 %copy-start.1 = (f32[256,1024]{1,0:T(8,128)S(1)}, f32[256,1024]{1,0:T(8,128)}, u32[]{:S(2)}) copy-start(f32[256,1024]{1,0:T(8,128)} %z_ref.7) | copy-start | bytes 3145732
  10.3 6.6 %collective-permute-start.1 = (f32[256,128]{1,0:T(8,128)S(1)}, f32[256,128]{1,0:T(8,128)S(1)}, u32[]{:S(2)}, u32[]{:S(2)}) collective-permute-start(f32[256,128]{1,0:T(8,128)S(1)} %get-tuple-element.52), channel_id=1, source_target_pairs={{0,12},{4,8},{8,4},{12,0},{16,28},{20,24},{24,20},{28,16},{1,13},{... | collective-permute-start | bytes 393224 | tf_op jit(solution)/shard_map/ppermute | solution.py:247
  17.0 4.7 %collective-permute-start.4 = (f32[256,128]{1,0:T(8,128)S(1)}, f32[256,128]{1,0:T(8,128)S(1)}, u32[]{:S(2)}, u32[]{:S(2)}) collective-permute-start(f32[256,128]{1,0:T(8,128)S(1)} %add_add_fusion), channel_id=1, source_target_pairs={{0,5},{1,7},{2,4},{3,6},{4,2},{5,0},{6,3},{7,1},{8,13},{9,15},{10,... | collective-permute-start | bytes 393224 | tf_op jit(solution)/shard_map/ppermute | solution.py:293
  21.7 6.8 %collective-permute-start.5 = (f32[256,128]{1,0:T(8,128)S(1)}, f32[256,128]{1,0:T(8,128)S(1)}, u32[]{:S(2)}, u32[]{:S(2)}) collective-permute-start(f32[256,128]{1,0:T(8,128)S(1)} %add.47.refs_0_), channel_id=1, source_target_pairs={{0,6},{1,4},{2,7},{3,5},{4,1},{5,3},{6,0},{7,2},{8,14},{9,12},{10,... | collective-permute-start | bytes 393224 | tf_op jit(solution)/shard_map/ppermute | solution.py:293
  28.9 5.1 %collective-permute-start.6 = (f32[256,128]{1,0:T(8,128)S(1)}, f32[256,128]{1,0:T(8,128)S(1)}, u32[]{:S(2)}, u32[]{:S(2)}) collective-permute-start(f32[256,128]{1,0:T(8,128)S(1)} %shard_map.44), channel_id=1, source_target_pairs={{0,12},{4,8},{8,4},{12,0},{16,28},{20,24},{24,20},{28,16},{1,13},{... | collective-permute-start | bytes 393224 | tf_op jit(solution)/shard_map/ppermute | solution.py:247
  34.0 3.3 %collective-permute-start.7 = (f32[2,256,128]{2,1,0:T(8,128)S(1)}, f32[2,256,128]{2,1,0:T(8,128)S(1)}, u32[]{:S(2)}, u32[]{:S(2)}) collective-permute-start(f32[2,256,128]{2,1,0:T(8,128)S(1)} %pad_maximum_fusion.near_ref), channel_id=1, source_target_pairs={{0,4},{4,0},{8,12},{12,8},{16,20},{20,16},{24,28},{28,24},{1,5},{5... | collective-permute-start | bytes 786440 | tf_op jit(solution)/shard_map/ppermute | solution.py:247
  34.7 6.5 %collective-permute-start.8 = (f32[256,128]{1,0:T(8,128)S(1)}, f32[256,128]{1,0:T(8,128)S(1)}, u32[]{:S(2)}, u32[]{:S(2)}) collective-permute-start(f32[256,128]{1,0:T(8,128)S(1)} %shard_map.44), channel_id=1, source_target_pairs={{0,28},{4,24},{8,20},{12,16},{16,12},{20,8},{24,4},{28,0},{1,29},{... | collective-permute-start | bytes 393224 | tf_op jit(solution)/shard_map/ppermute | solution.py:247
  35.9 8.3 %collective-permute-start.9 = (f32[256,128]{1,0:T(8,128)S(1)}, f32[256,128]{1,0:T(8,128)S(1)}, u32[]{:S(2)}, u32[]{:S(2)}) collective-permute-start(f32[256,128]{1,0:T(8,128)S(1)} %shard_map.44), channel_id=1, source_target_pairs={{0,20},{4,16},{8,28},{12,24},{16,4},{20,0},{24,12},{28,8},{1,21},{... | collective-permute-start | bytes 393224 | tf_op jit(solution)/shard_map/ppermute | solution.py:247
  44.1 1.6 %collective-permute-start.10 = (f32[2,256,128]{2,1,0:T(8,128)S(1)}, f32[2,256,128]{2,1,0:T(8,128)S(1)}, u32[]{:S(2)}, u32[]{:S(2)}) collective-permute-start(f32[2,256,128]{2,1,0:T(8,128)S(1)} %pad_maximum_fusion.1.near_ref), channel_id=1, source_target_pairs={{0,4},{4,0},{8,12},{12,8},{16,20},{20,16},{24,28},{28,24},{1,5},{5... | collective-permute-start | bytes 786440 | tf_op jit(solution)/shard_map/ppermute | solution.py:247
